TPU v7x, 128 devices: a whole 4x4x4 slice. The times are simulated.
128 devices in a mesh: row: 16 (over x, y), col: 8 (over z, core).
Axes of the slice: x: 4, y: 4, z: 4, core: 2. Of those that a mesh axis runs over, the one named last changes fastest.
Arguments:
- tokens: bfloat16 [32, 8192], P(None, 'row'), may hold values from -6 to 6
- gain: float32 [8192], P('row'), may hold values from 0.24 to 4.5
- gate_weight: bfloat16 [8192, 28672], P('row', 'col'), may hold values from -0.0625 to 0.0625
- up_weight: bfloat16 [8192, 28672], P('row', 'col'), may hold values from -0.0625 to 0.0625
- down_weight: bfloat16 [28672, 8192], P('col', 'row'), may hold values from -0.03125 to 0.03125
- probes: float32 [4, 32, 8192], P(None, None, 'row'), may hold values from -6 to 6
Outputs:
- basis: float32 [4, 32, 8192], P(None, None, 'row')
- stretch: float32 [4], replicated
All inputs are finite; a program needn't handle non-finite values.
Results may differ from a plain program's by a relative error of at most 0.0085.
Values may be sent and summed in bfloat16 or wider, within the bound.
A program may use at most 64 MiB of HBM per device.

v0:
```python
import functools
import jax
import jax.numpy as jnp
from jax import lax
from jax.sharding import Mesh
from jax.sharding import PartitionSpec as P

ITERS = 3
ROW = ("row_0", "row_1")
epsilon = 1e-06


def in_blocks(array, dim, count):
    dims = array.shape
    parts = array.reshape(*dims[:dim], count, dims[dim] // count, *dims[dim + 1 :])
    return jnp.moveaxis(parts, dim, 0)


def summed_on_arrival(array, axis, dim):
    count = lax.axis_size(axis)
    parts = lax.all_to_all(in_blocks(array, dim, count), axis, 0, 0, tiled=True)
    return jnp.sum(parts, axis=0)


def from_everyone(array, axis):
    copies = jnp.broadcast_to(array, (lax.axis_size(axis), *array.shape))
    return lax.all_to_all(copies, axis, split_axis=0, concat_axis=0, tiled=True)


def joined_along(parts, dim):
    dims = list(parts.shape[1:])
    dims[dim] *= parts.shape[0]
    return jnp.moveaxis(parts, 0, dim).reshape(dims)


def gather_directly(array, axis, dim):
    parts = from_everyone(array, axis)
    return joined_along(parts, dim)


def of_everyone(array, axis):
    return from_everyone(array, axis).sum(axis=0)


def by_axis(array, axes):
    return functools.reduce(lax.psum, axes, array)


def local(tokens, gain, gate_weight, up_weight, down_weight, probes):
    scaled = (tokens.astype(jnp.float32) * gain).astype(jnp.bfloat16)
    gate_part = jnp.dot(scaled, gate_weight, preferred_element_type=jnp.float32)
    up_part = jnp.dot(scaled, up_weight, preferred_element_type=jnp.float32)
    gate, up = lax.psum((gate_part, up_part), ROW)
    sigmoid_gate = 1.0 / (1.0 + jnp.exp(-gate))
    activated = gate * sigmoid_gate
    slope = sigmoid_gate * (1.0 + gate * (1.0 - sigmoid_gate)) * up
    probe_count, token_count, local_width = probes.shape
    row_count = probe_count * token_count
    slope_all = jnp.tile(slope, (probe_count, 1))
    activated_all = jnp.tile(activated, (probe_count, 1))
    entries = token_count * local_width * lax.axis_size(ROW)
    transposed = (((1,), (1,)), ((), ()))
    current = probes
    level = jnp.zeros((probe_count,), jnp.float32)
    for sweep in range(ITERS):
        pushed = (current * gain).astype(jnp.bfloat16).reshape(row_count, local_width)
        gate_tan = jnp.dot(pushed, gate_weight, preferred_element_type=jnp.float32)
        up_tan = jnp.dot(pushed, up_weight, preferred_element_type=jnp.float32)
        joined = slope_all * gate_tan + activated_all * up_tan
        hidden = summed_on_arrival(joined, ROW, 0).astype(jnp.bfloat16)
        tangent_part = jnp.dot(
            gather_directly(hidden, ROW, 0), down_weight, preferred_element_type=jnp.float32
        )
        tangent = of_everyone(tangent_part, "col").astype(jnp.bfloat16)
        back_part = lax.dot_general(
            tangent, down_weight, transposed, preferred_element_type=jnp.float32
        )
        back_share = summed_on_arrival(back_part, ROW, 0).astype(jnp.bfloat16)
        piece = gather_directly(back_share, ROW, 0)
        gate_pull = (slope_all * piece).astype(jnp.bfloat16)
        up_pull = (activated_all * piece).astype(jnp.bfloat16)
        result = lax.dot_general(
            gate_pull, gate_weight, transposed, preferred_element_type=jnp.float32
        )
        pulled_part = result + lax.dot_general(
            up_pull, up_weight, transposed, preferred_element_type=jnp.float32
        )
        pulled = of_everyone(pulled_part, "col")
        grown = pulled.reshape(probe_count, token_count, local_width) * gain
        squares = jnp.sum(grown * grown, axis=(1, 2))
        level = by_axis(squares, ROW) / entries
        current = grown * lax.rsqrt(level + epsilon)[:, None, None]
    return (current, jnp.sqrt(level))


def solution(mesh):
    torus = Mesh(mesh.devices.reshape(4, 4, mesh.shape["col"]), ("row_0", "row_1", "col"))
    in_specs = (
        P(None, ROW),
        P(ROW),
        P(ROW, "col"),
        P(ROW, "col"),
        P("col", ROW),
        P(None, None, ROW),
    )
    out_specs = (P(None, None, ROW), P())
    return jax.shard_map(local, mesh=torus, in_specs=in_specs, out_specs=out_specs, check_vma=False)
```

profile of v0, /device:TPU:0, one launch (start us, length us, event | category | flops | bytes accessed | tf_op | source)
XLA Modules:
  0.0 655.0 jit_solution(17898869282795394094)
XLA Ops:
  12.6 88.8 %all-reduce.3.cloned.1.call-done = (f32[32,3584]{1,0:T(8,128)}, f32[32,3584]{1,0:T(8,128)}) async-done(((f32[32,3584]{1,0:T(8,128)}, f32[32,3584]{1,0:T(8,128)}), (f32[32,3584]{1,0:T(8,128)}, f32[32,3584]{1,0:T(8,128)})) %all-reduce.3.cloned.1.call-update) | async-done | bytes 917520 | tf_op jit(solution)/shard_map/psum | solution.py:53
  106.6 28.0 %all_to_all.90 = f32[16,8,3584]{2,1,0:T(8,128)S(1)} all-to-all(f32[16,8,3584]{2,1,0:T(8,128)S(1)} %fusion.3), channel_id=1, replica_groups=mesh['row_0'=4,'row_1'=4,'col'=8] {'row_0','row_1'}, dimensions={0} | all-to-all | bytes 3670016 | tf_op jit(solution)/shard_map/all_to_all | solution.py:21
  134.8 15.7 %all_to_all.91 = bf16[16,8,3584]{2,1,0:T(8,128)(2,1)S(1)} all-to-all(bf16[16,8,3584]{2,1,0:T(8,128)(2,1)S(1)} %broadcast_in_dim.46), channel_id=1, replica_groups=mesh['row_0'=4,'row_1'=4,'col'=8] {'row_0','row_1'}, dimensions={0} | all-to-all | bytes 1835008 | tf_op jit(solution)/shard_map/all_to_all | solution.py:27
  153.4 31.4 %all_to_all.92 = f32[8,128,512]{2,1,0:T(8,128)S(1)} all-to-all(f32[8,128,512]{2,1,0:T(8,128)S(1)} %broadcast_in_dim.47), channel_id=1, replica_groups=mesh['row_0'=4,'row_1'=4,'col'=8] {'col'}, dimensions={0} | all-to-all | bytes 4194304 | tf_op jit(solution)/shard_map/all_to_all | solution.py:27
  188.4 28.5 %all_to_all.93 = f32[16,8,3584]{2,1,0:T(8,128)S(1)} all-to-all(f32[16,8,3584]{2,1,0:T(8,128)S(1)} %convolution_bitcast_fusion.2), channel_id=1, replica_groups=mesh['row_0'=4,'row_1'=4,'col'=8] {'row_0','row_1'}, dimensions={0} | all-to-all | bytes 3670016 | tf_op jit(solution)/shard_map/all_to_all | solution.py:21
  217.1 17.2 %all_to_all.94 = bf16[16,8,3584]{2,1,0:T(8,128)(2,1)S(1)} all-to-all(bf16[16,8,3584]{2,1,0:T(8,128)(2,1)S(1)} %broadcast_in_dim.48), channel_id=1, replica_groups=mesh['row_0'=4,'row_1'=4,'col'=8] {'row_0','row_1'}, dimensions={0} | all-to-all | bytes 1835008 | tf_op jit(solution)/shard_map/all_to_all | solution.py:27
  239.9 30.2 %all_to_all.95 = f32[8,128,512]{2,1,0:T(8,128)S(1)} all-to-all(f32[8,128,512]{2,1,0:T(8,128)S(1)} %broadcast_in_dim.49), channel_id=1, replica_groups=mesh['row_0'=4,'row_1'=4,'col'=8] {'col'}, dimensions={0} | all-to-all | bytes 4194304 | tf_op jit(solution)/shard_map/all_to_all | solution.py:27
  270.7 9.0 %psum.58 = f32[4]{0:T(128)S(1)} all-reduce(f32[4]{0:T(128)S(1)} %reduce_sum.162), channel_id=1, replica_groups=mesh['row_0'=4,'row_1'=4,'col'=8] {'row_0'}, use_global_device_ids=true, to_apply=%region_8.0 | all-reduce | flops 4 | bytes 32 | tf_op jit(solution)/shard_map/psum | solution.py:46
  292.1 24.0 %all_to_all.96 = f32[16,8,3584]{2,1,0:T(8,128)S(1)} all-to-all(f32[16,8,3584]{2,1,0:T(8,128)S(1)} %fusion.4), channel_id=1, replica_groups=mesh['row_0'=4,'row_1'=4,'col'=8] {'row_0','row_1'}, dimensions={0} | all-to-all | bytes 3670016 | tf_op jit(solution)/shard_map/all_to_all | solution.py:21
  316.3 15.5 %all_to_all.97 = bf16[16,8,3584]{2,1,0:T(8,128)(2,1)S(1)} all-to-all(bf16[16,8,3584]{2,1,0:T(8,128)(2,1)S(1)} %broadcast_in_dim.50), channel_id=1, replica_groups=mesh['row_0'=4,'row_1'=4,'col'=8] {'row_0','row_1'}, dimensions={0} | all-to-all | bytes 1835008 | tf_op jit(solution)/shard_map/all_to_all | solution.py:27
  334.7 29.7 %all_to_all.98 = f32[8,128,512]{2,1,0:T(8,128)S(1)} all-to-all(f32[8,128,512]{2,1,0:T(8,128)S(1)} %broadcast_in_dim.51), channel_id=1, replica_groups=mesh['row_0'=4,'row_1'=4,'col'=8] {'col'}, dimensions={0} | all-to-all | bytes 4194304 | tf_op jit(solution)/shard_map/all_to_all | solution.py:27
  367.9 28.5 %all_to_all.99 = f32[16,8,3584]{2,1,0:T(8,128)S(1)} all-to-all(f32[16,8,3584]{2,1,0:T(8,128)S(1)} %convolution_bitcast_fusion.1), channel_id=1, replica_groups=mesh['row_0'=4,'row_1'=4,'col'=8] {'row_0','row_1'}, dimensions={0} | all-to-all | bytes 3670016 | tf_op jit(solution)/shard_map/all_to_all | solution.py:21
  396.5 17.4 %all_to_all.100 = bf16[16,8,3584]{2,1,0:T(8,128)(2,1)S(1)} all-to-all(bf16[16,8,3584]{2,1,0:T(8,128)(2,1)S(1)} %broadcast_in_dim.52), channel_id=1, replica_groups=mesh['row_0'=4,'row_1'=4,'col'=8] {'row_0','row_1'}, dimensions={0} | all-to-all | bytes 1835008 | tf_op jit(solution)/shard_map/all_to_all | solution.py:27
  419.6 29.9 %all_to_all.101 = f32[8,128,512]{2,1,0:T(8,128)S(1)} all-to-all(f32[8,128,512]{2,1,0:T(8,128)S(1)} %broadcast_in_dim.53), channel_id=1, replica_groups=mesh['row_0'=4,'row_1'=4,'col'=8] {'col'}, dimensions={0} | all-to-all | bytes 4194304 | tf_op jit(solution)/shard_map/all_to_all | solution.py:27
  450.1 9.0 %psum.60 = f32[4]{0:T(128)S(1)} all-reduce(f32[4]{0:T(128)S(1)} %reduce_sum.169), channel_id=1, replica_groups=mesh['row_0'=4,'row_1'=4,'col'=8] {'row_0'}, use_global_device_ids=true, to_apply=%region_16.0 | all-reduce | flops 4 | bytes 32 | tf_op jit(solution)/shard_map/psum | solution.py:46
  459.1 8.4 %psum.61 = f32[4]{0:T(128)S(1)} all-reduce(f32[4]{0:T(128)S(1)} %psum.60), channel_id=1, replica_groups=mesh['row_0'=4,'row_1'=4,'col'=8] {'row_1'}, use_global_device_ids=true, to_apply=%region_17.0 | all-reduce | flops 4 | bytes 32 | tf_op jit(solution)/shard_map/psum | solution.py:46
  471.5 24.0 %all_to_all.102 = f32[16,8,3584]{2,1,0:T(8,128)S(1)} all-to-all(f32[16,8,3584]{2,1,0:T(8,128)S(1)} %fusion.5), channel_id=1, replica_groups=mesh['row_0'=4,'row_1'=4,'col'=8] {'row_0','row_1'}, dimensions={0} | all-to-all | bytes 3670016 | tf_op jit(solution)/shard_map/all_to_all | solution.py:21
  495.6 15.5 %all_to_all.103 = bf16[16,8,3584]{2,1,0:T(8,128)(2,1)S(1)} all-to-all(bf16[16,8,3584]{2,1,0:T(8,128)(2,1)S(1)} %broadcast_in_dim.54), channel_id=1, replica_groups=mesh['row_0'=4,'row_1'=4,'col'=8] {'row_0','row_1'}, dimensions={0} | all-to-all | bytes 1835008 | tf_op jit(solution)/shard_map/all_to_all | solution.py:27
  514.0 29.7 %all_to_all.104 = f32[8,128,512]{2,1,0:T(8,128)S(1)} all-to-all(f32[8,128,512]{2,1,0:T(8,128)S(1)} %broadcast_in_dim.55), channel_id=1, replica_groups=mesh['row_0'=4,'row_1'=4,'col'=8] {'col'}, dimensions={0} | all-to-all | bytes 4194304 | tf_op jit(solution)/shard_map/all_to_all | solution.py:27
  547.2 28.5 %all_to_all.105 = f32[16,8,3584]{2,1,0:T(8,128)S(1)} all-to-all(f32[16,8,3584]{2,1,0:T(8,128)S(1)} %convolution_bitcast_fusion), channel_id=1, replica_groups=mesh['row_0'=4,'row_1'=4,'col'=8] {'row_0','row_1'}, dimensions={0} | all-to-all | bytes 3670016 | tf_op jit(solution)/shard_map/all_to_all | solution.py:21
  575.9 17.4 %all_to_all.106 = bf16[16,8,3584]{2,1,0:T(8,128)(2,1)S(1)} all-to-all(bf16[16,8,3584]{2,1,0:T(8,128)(2,1)S(1)} %broadcast_in_dim.56), channel_id=1, replica_groups=mesh['row_0'=4,'row_1'=4,'col'=8] {'row_0','row_1'}, dimensions={0} | all-to-all | bytes 1835008 | tf_op jit(solution)/shard_map/all_to_all | solution.py:27
  599.0 29.9 %all_to_all.107 = f32[8,128,512]{2,1,0:T(8,128)S(1)} all-to-all(f32[8,128,512]{2,1,0:T(8,128)S(1)} %broadcast_in_dim.57), channel_id=1, replica_groups=mesh['row_0'=4,'row_1'=4,'col'=8] {'col'}, dimensions={0} | all-to-all | bytes 4194304 | tf_op jit(solution)/shard_map/all_to_all | solution.py:27
  629.4 9.0 %psum.62 = f32[4]{0:T(128)S(1)} all-reduce(f32[4]{0:T(128)S(1)} %reduce_sum.176), channel_id=1, replica_groups=mesh['row_0'=4,'row_1'=4,'col'=8] {'row_0'}, use_global_device_ids=true, to_apply=%region_24.25 | all-reduce | flops 4 | bytes 32 | tf_op jit(solution)/shard_map/psum | solution.py:46
  638.4 8.4 %psum.63 = f32[4]{0:T(128)S(1)} all-reduce(f32[4]{0:T(128)S(1)} %psum.62), channel_id=1, replica_groups=mesh['row_0'=4,'row_1'=4,'col'=8] {'row_1'}, use_global_device_ids=true, to_apply=%region_25.26 | all-reduce | flops 4 | bytes 32 | tf_op jit(solution)/shard_map/psum | solution.py:46
  (95 shorter events, 67.0 us)
Async XLA Ops:
  7.2 3.8 copy-start.11
  7.2 3.8 copy-start.12
  7.2 94.2 %all-reduce.3.cloned.1.call-start = ((), (), s32[]{:S(2)}) async-start(), calls=%async_computation.18 | async-start | bytes 1835008 | tf_op jit(solution)/shard_map/psum | solution.py:53
  7.2 3.8 copy-start.6
  11.0 1.6 copy-start.10
  102.7 3.1 copy-start
  234.3 2.0 copy-start.7
  236.3 2.0 copy-start.1
  288.3 3.1 copy-start.2
  414.0 2.0 copy-start.8
  416.0 2.0 copy-start.3
  467.6 3.1 copy-start.4
  593.3 2.0 copy-start.9
  595.4 2.0 copy-start.5
Sparse Core Ops, SparseCore 0:
  12.7 88.6 all-reduce.2
where the time goes:
time: 656 us; the launch traced here: 655 us
  blocking collectives  493 us (75%)
  waiting for transfers between devices  88.8 us (14%)
  matrix products  41.8 us (6%)
  between operations  14.4 us (2%)
  local copies, waits for them, and re-layouts  10.8 us (2%)
    all_to_all x12, blocking collectives, from_everyone(): return lax.all_to_all(copies, axis, split_axis=0, concat_axis=0, tiled=True)  279 us
    all_to_all x6, blocking collectives, summed_on_arrival(): parts = lax.all_to_all(in_blocks(array, dim, count), axis, 0, 0, tiled=True)  161 us
    psum x1, waiting for transfers between devices, local(): gate, up = lax.psum((gate_part, up_part), ROW)  88.8 us
    psum x6, blocking collectives, by_axis(): return functools.reduce(lax.psum, axes, array)  52.2 us
  transfers between devices with their start and end apart: 1, of which 1 were waited for; matrix products, arithmetic and copies ran while one was open for 0% of the time, Pallas kernels for 0%

commit v1 on v0

--- a/solution.py
+++ b/solution.py
@@ -50,7 +50,7 @@
     scaled = (tokens.astype(jnp.float32) * gain).astype(jnp.bfloat16)
     gate_part = jnp.dot(scaled, gate_weight, preferred_element_type=jnp.float32)
     up_part = jnp.dot(scaled, up_weight, preferred_element_type=jnp.float32)
-    gate, up = lax.psum((gate_part, up_part), ROW)
+    gate, up = lax.psum(lax.psum((gate_part, up_part), "row_0"), "row_1")
     sigmoid_gate = 1.0 / (1.0 + jnp.exp(-gate))
     activated = gate * sigmoid_gate
     slope = sigmoid_gate * (1.0 + gate * (1.0 - sigmoid_gate)) * up

time: 656 us -> 665 us (1.014)
  waiting for transfers between devices: 88.8 us -> 96.4 us
    psum x1 -> x2, waiting for transfers between devices: 88.8 us -> 96.4 us  [local(): gate, up = lax.psum(lax.psum((gate_part, up_part), 'row_0'), 'row_1')]
  transfers between devices with their start and end apart: 1 -> 2, of which waited for: 1 -> 2; matrix products, arithmetic and copies ran while one was open for 0% -> 0% of each run, Pallas kernels for 0% -> 0%
where the time goes in v1:
time: 665 us; the launch traced here: 664 us
  blocking collectives  494 us (74%)
  waiting for transfers between devices  96.4 us (14%)
  matrix products  41.8 us (6%)
  between operations  14.4 us (2%)
  local copies, waits for them, and re-layouts  10.8 us (2%)
    all_to_all x12, blocking collectives, from_everyone(): return lax.all_to_all(copies, axis, split_axis=0, concat_axis=0, tiled=True)  279 us
    all_to_all x6, blocking collectives, summed_on_arrival(): parts = lax.all_to_all(in_blocks(array, dim, count), axis, 0, 0, tiled=True)  163 us
    psum x2, waiting for transfers between devices, local(): gate, up = lax.psum(lax.psum((gate_part, up_part), 'row_0'), 'row_1')  96.4 us
    psum x6, blocking collectives, by_axis(): return functools.reduce(lax.psum, axes, array)  52.2 us
  transfers between devices with their start and end apart: 2, of which 2 were waited for; matrix products, arithmetic and copies ran while one was open for 0% of the time, Pallas kernels for 0%

profile of v1, /device:TPU:0, one launch (start us, length us, event | category | flops | bytes accessed | tf_op | source)
XLA Modules:
  0.0 663.9 jit_solution(16714811177965980441)
XLA Ops:
  12.6 47.8 %all-reduce.7.cloned.1.call-done = (f32[32,3584]{1,0:T(8,128)}, f32[32,3584]{1,0:T(8,128)}) async-done(((f32[32,3584]{1,0:T(8,128)}, f32[32,3584]{1,0:T(8,128)}), (f32[32,3584]{1,0:T(8,128)}, f32[32,3584]{1,0:T(8,128)})) %all-reduce.7.cloned.1.call-update) | async-done | bytes 917520 | tf_op jit(solution)/shard_map/psum | solution.py:53
  60.5 48.6 %all-reduce.5.cloned.1.call-done = (f32[32,3584]{1,0:T(8,128)}, f32[32,3584]{1,0:T(8,128)}) async-done(((f32[32,3584]{1,0:T(8,128)}, f32[32,3584]{1,0:T(8,128)}), (f32[32,3584]{1,0:T(8,128)}, f32[32,3584]{1,0:T(8,128)})) %all-reduce.5.cloned.1.call-update) | async-done | bytes 917520 | tf_op jit(solution)/shard_map/psum | solution.py:53
  114.3 29.4 %all_to_all.90 = f32[16,8,3584]{2,1,0:T(8,128)S(1)} all-to-all(f32[16,8,3584]{2,1,0:T(8,128)S(1)} %fusion.3), channel_id=1, replica_groups=mesh['row_0'=4,'row_1'=4,'col'=8] {'row_0','row_1'}, dimensions={0} | all-to-all | bytes 3670016 | tf_op jit(solution)/shard_map/all_to_all | solution.py:21
  143.8 15.5 %all_to_all.91 = bf16[16,8,3584]{2,1,0:T(8,128)(2,1)S(1)} all-to-all(bf16[16,8,3584]{2,1,0:T(8,128)(2,1)S(1)} %broadcast_in_dim.46), channel_id=1, replica_groups=mesh['row_0'=4,'row_1'=4,'col'=8] {'row_0','row_1'}, dimensions={0} | all-to-all | bytes 1835008 | tf_op jit(solution)/shard_map/all_to_all | solution.py:27
  162.3 31.4 %all_to_all.92 = f32[8,128,512]{2,1,0:T(8,128)S(1)} all-to-all(f32[8,128,512]{2,1,0:T(8,128)S(1)} %broadcast_in_dim.47), channel_id=1, replica_groups=mesh['row_0'=4,'row_1'=4,'col'=8] {'col'}, dimensions={0} | all-to-all | bytes 4194304 | tf_op jit(solution)/shard_map/all_to_all | solution.py:27
  197.3 28.5 %all_to_all.93 = f32[16,8,3584]{2,1,0:T(8,128)S(1)} all-to-all(f32[16,8,3584]{2,1,0:T(8,128)S(1)} %convolution_bitcast_fusion.2), channel_id=1, replica_groups=mesh['row_0'=4,'row_1'=4,'col'=8] {'row_0','row_1'}, dimensions={0} | all-to-all | bytes 3670016 | tf_op jit(solution)/shard_map/all_to_all | solution.py:21
  226.0 17.4 %all_to_all.94 = bf16[16,8,3584]{2,1,0:T(8,128)(2,1)S(1)} all-to-all(bf16[16,8,3584]{2,1,0:T(8,128)(2,1)S(1)} %broadcast_in_dim.48), channel_id=1, replica_groups=mesh['row_0'=4,'row_1'=4,'col'=8] {'row_0','row_1'}, dimensions={0} | all-to-all | bytes 1835008 | tf_op jit(solution)/shard_map/all_to_all | solution.py:27
  249.0 30.0 %all_to_all.95 = f32[8,128,512]{2,1,0:T(8,128)S(1)} all-to-all(f32[8,128,512]{2,1,0:T(8,128)S(1)} %broadcast_in_dim.49), channel_id=1, replica_groups=mesh['row_0'=4,'row_1'=4,'col'=8] {'col'}, dimensions={0} | all-to-all | bytes 4194304 | tf_op jit(solution)/shard_map/all_to_all | solution.py:27
  279.6 9.0 %psum.74 = f32[4]{0:T(128)S(1)} all-reduce(f32[4]{0:T(128)S(1)} %reduce_sum.162), channel_id=1, replica_groups=mesh['row_0'=4,'row_1'=4,'col'=8] {'row_0'}, use_global_device_ids=true, to_apply=%region_10.0 | all-reduce | flops 4 | bytes 32 | tf_op jit(solution)/shard_map/psum | solution.py:46
  301.0 24.0 %all_to_all.96 = f32[16,8,3584]{2,1,0:T(8,128)S(1)} all-to-all(f32[16,8,3584]{2,1,0:T(8,128)S(1)} %fusion.4), channel_id=1, replica_groups=mesh['row_0'=4,'row_1'=4,'col'=8] {'row_0','row_1'}, dimensions={0} | all-to-all | bytes 3670016 | tf_op jit(solution)/shard_map/all_to_all | solution.py:21
  325.1 15.5 %all_to_all.97 = bf16[16,8,3584]{2,1,0:T(8,128)(2,1)S(1)} all-to-all(bf16[16,8,3584]{2,1,0:T(8,128)(2,1)S(1)} %broadcast_in_dim.50), channel_id=1, replica_groups=mesh['row_0'=4,'row_1'=4,'col'=8] {'row_0','row_1'}, dimensions={0} | all-to-all | bytes 1835008 | tf_op jit(solution)/shard_map/all_to_all | solution.py:27
  343.6 29.7 %all_to_all.98 = f32[8,128,512]{2,1,0:T(8,128)S(1)} all-to-all(f32[8,128,512]{2,1,0:T(8,128)S(1)} %broadcast_in_dim.51), channel_id=1, replica_groups=mesh['row_0'=4,'row_1'=4,'col'=8] {'col'}, dimensions={0} | all-to-all | bytes 4194304 | tf_op jit(solution)/shard_map/all_to_all | solution.py:27
  376.8 28.5 %all_to_all.99 = f32[16,8,3584]{2,1,0:T(8,128)S(1)} all-to-all(f32[16,8,3584]{2,1,0:T(8,128)S(1)} %convolution_bitcast_fusion.1), channel_id=1, replica_groups=mesh['row_0'=4,'row_1'=4,'col'=8] {'row_0','row_1'}, dimensions={0} | all-to-all | bytes 3670016 | tf_op jit(solution)/shard_map/all_to_all | solution.py:21
  405.4 17.4 %all_to_all.100 = bf16[16,8,3584]{2,1,0:T(8,128)(2,1)S(1)} all-to-all(bf16[16,8,3584]{2,1,0:T(8,128)(2,1)S(1)} %broadcast_in_dim.52), channel_id=1, replica_groups=mesh['row_0'=4,'row_1'=4,'col'=8] {'row_0','row_1'}, dimensions={0} | all-to-all | bytes 1835008 | tf_op jit(solution)/shard_map/all_to_all | solution.py:27
  428.5 29.9 %all_to_all.101 = f32[8,128,512]{2,1,0:T(8,128)S(1)} all-to-all(f32[8,128,512]{2,1,0:T(8,128)S(1)} %broadcast_in_dim.53), channel_id=1, replica_groups=mesh['row_0'=4,'row_1'=4,'col'=8] {'col'}, dimensions={0} | all-to-all | bytes 4194304 | tf_op jit(solution)/shard_map/all_to_all | solution.py:27
  459.0 9.0 %psum.76 = f32[4]{0:T(128)S(1)} all-reduce(f32[4]{0:T(128)S(1)} %reduce_sum.169), channel_id=1, replica_groups=mesh['row_0'=4,'row_1'=4,'col'=8] {'row_0'}, use_global_device_ids=true, to_apply=%region_18.0 | all-reduce | flops 4 | bytes 32 | tf_op jit(solution)/shard_map/psum | solution.py:46
  467.9 8.4 %psum.77 = f32[4]{0:T(128)S(1)} all-reduce(f32[4]{0:T(128)S(1)} %psum.76), channel_id=1, replica_groups=mesh['row_0'=4,'row_1'=4,'col'=8] {'row_1'}, use_global_device_ids=true, to_apply=%region_19.0 | all-reduce | flops 4 | bytes 32 | tf_op jit(solution)/shard_map/psum | solution.py:46
  480.4 24.0 %all_to_all.102 = f32[16,8,3584]{2,1,0:T(8,128)S(1)} all-to-all(f32[16,8,3584]{2,1,0:T(8,128)S(1)} %fusion.5), channel_id=1, replica_groups=mesh['row_0'=4,'row_1'=4,'col'=8] {'row_0','row_1'}, dimensions={0} | all-to-all | bytes 3670016 | tf_op jit(solution)/shard_map/all_to_all | solution.py:21
  504.5 15.5 %all_to_all.103 = bf16[16,8,3584]{2,1,0:T(8,128)(2,1)S(1)} all-to-all(bf16[16,8,3584]{2,1,0:T(8,128)(2,1)S(1)} %broadcast_in_dim.54), channel_id=1, replica_groups=mesh['row_0'=4,'row_1'=4,'col'=8] {'row_0','row_1'}, dimensions={0} | all-to-all | bytes 1835008 | tf_op jit(solution)/shard_map/all_to_all | solution.py:27
  522.9 29.7 %all_to_all.104 = f32[8,128,512]{2,1,0:T(8,128)S(1)} all-to-all(f32[8,128,512]{2,1,0:T(8,128)S(1)} %broadcast_in_dim.55), channel_id=1, replica_groups=mesh['row_0'=4,'row_1'=4,'col'=8] {'col'}, dimensions={0} | all-to-all | bytes 4194304 | tf_op jit(solution)/shard_map/all_to_all | solution.py:27
  556.1 28.5 %all_to_all.105 = f32[16,8,3584]{2,1,0:T(8,128)S(1)} all-to-all(f32[16,8,3584]{2,1,0:T(8,128)S(1)} %convolution_bitcast_fusion), channel_id=1, replica_groups=mesh['row_0'=4,'row_1'=4,'col'=8] {'row_0','row_1'}, dimensions={0} | all-to-all | bytes 3670016 | tf_op jit(solution)/shard_map/all_to_all | solution.py:21
  584.8 17.4 %all_to_all.106 = bf16[16,8,3584]{2,1,0:T(8,128)(2,1)S(1)} all-to-all(bf16[16,8,3584]{2,1,0:T(8,128)(2,1)S(1)} %broadcast_in_dim.56), channel_id=1, replica_groups=mesh['row_0'=4,'row_1'=4,'col'=8] {'row_0','row_1'}, dimensions={0} | all-to-all | bytes 1835008 | tf_op jit(solution)/shard_map/all_to_all | solution.py:27
  607.9 29.9 %all_to_all.107 = f32[8,128,512]{2,1,0:T(8,128)S(1)} all-to-all(f32[8,128,512]{2,1,0:T(8,128)S(1)} %broadcast_in_dim.57), channel_id=1, replica_groups=mesh['row_0'=4,'row_1'=4,'col'=8] {'col'}, dimensions={0} | all-to-all | bytes 4194304 | tf_op jit(solution)/shard_map/all_to_all | solution.py:27
  638.3 9.0 %psum.78 = f32[4]{0:T(128)S(1)} all-reduce(f32[4]{0:T(128)S(1)} %reduce_sum.176), channel_id=1, replica_groups=mesh['row_0'=4,'row_1'=4,'col'=8] {'row_0'}, use_global_device_ids=true, to_apply=%region_26.27 | all-reduce | flops 4 | bytes 32 | tf_op jit(solution)/shard_map/psum | solution.py:46
  (98 shorter events, 75.5 us)
Async XLA Ops:
  7.2 3.8 copy-start.11
  7.2 3.8 copy-start.12
  7.2 53.2 %all-reduce.7.cloned.1.call-start = ((), (), s32[]{:S(2)}) async-start(), calls=%async_computation.19 | async-start | bytes 1835008 | tf_op jit(solution)/shard_map/psum | solution.py:53
  7.2 3.8 copy-start.6
  11.0 49.4 %copy-start.10 = (f32[4,32,512]{2,1,0:T(8,128)S(1)}, f32[4,32,512]{2,1,0:T(8,128)}, u32[]{:S(2)}) copy-start(f32[4,32,512]{2,1,0:T(8,128)} %param.11) | copy-start | bytes 786436
  12.6 96.5 %all-reduce.5.cloned.1.call-start = ((), (), s32[]{:S(2)}) async-start(), calls=%async_computation.18 | async-start | bytes 1835008 | tf_op jit(solution)/shard_map/psum | solution.py:53
  110.4 3.1 copy-start
  243.4 2.0 copy-start.7
  245.4 2.0 copy-start.1
  297.2 3.1 copy-start.2
  422.9 2.0 copy-start.8
  424.9 2.0 copy-start.3
  476.5 3.1 copy-start.4
  602.2 2.0 copy-start.9
  604.3 2.0 copy-start.5
Sparse Core Ops, SparseCore 0:
  12.7 47.6 all-reduce.6
  62.8 46.2 all-reduce.4
